TPU v7x, 128 devices: a whole 4x4x4 slice. The times are simulated.
128 devices in a mesh: wide: 64 (over x, z, y), narrow: 2 (over core).
Axes of the slice: x: 4, y: 4, z: 4, core: 2. Of those that a mesh axis runs over, the one named last changes fastest.
Arguments:
- contributions: float32 [2, 3, 32768, 128], P('narrow', None, 'wide'), may hold values from -6 to 6
- send_map: int32 [64, 896], P('wide'), may hold values from -1 to 511, as said below
- arrival_map: int32 [64, 896], P('wide'), may hold values from -1 to 255, as said below
- dual_diagonal: float32 [16384, 128], P('wide'), may hold values from 0.5 to 2
- mortar: bfloat16 [16384, 128, 128], P('wide'), may hold values from -0.5 to 0.5
- master_inverse: bfloat16 [16384, 128, 128], P('wide'), may hold values from -0.5 to 0.5
Outputs:
- corrections: float32 [2, 3, 32768, 128], P('narrow', None, 'wide')
Inputs may be any that keep to these rules, and one draw needn't show every extreme that they name: `send_map`: each row 0 to 511 of a partition stands in exactly one of its slots. Some stripe has all 14 of its slots used by every partition. arrival_map[d, o * 14 + c] is -1 exactly where send_map[o, d * 14 + c] is -1.
All inputs are finite; a program needn't handle non-finite values.
Results may differ from a plain program's by a relative error of at most 0.0041.
Values sent between devices are 32-bit elements; how exact they have to be, the bound alone decides.
A program may use at most 64 MiB of HBM per device.

v0:
```python
import jax
import jax.numpy as jnp
from jax import lax
from jax.sharding import PartitionSpec as P


def in_blocks(shard, dim, devices):
    shape = shard.shape
    pieces = shard.reshape(*shape[:dim], devices, shape[dim] // devices, *shape[dim + 1 :])
    return jnp.moveaxis(pieces, dim, 0)


def sent_and_summed(shard, axis, dim):
    pieces = in_blocks(shard, dim, lax.axis_size(axis))
    arrived = lax.all_to_all(pieces, axis, split_axis=0, concat_axis=0, tiled=True)
    return arrived.sum(axis=0)


def sent_to_all(shard, axis):
    copies = jnp.broadcast_to(shard, (lax.axis_size(axis), *shard.shape))
    return lax.all_to_all(copies, axis, split_axis=0, concat_axis=0, tiled=True)


def in_order(pieces, dim):
    shape = list(pieces.shape[1:])
    shape[dim] *= pieces.shape[0]
    return jnp.moveaxis(pieces, 0, dim).reshape(shape)


def gather_directly(shard, axis, dim):
    pieces = sent_to_all(shard, axis)
    return in_order(pieces, dim)


def condense(slave_sums, master_sums, diagonal, mortar_part, inverse_part):
    multiplier_low = (slave_sums / diagonal[None]).astype(jnp.bfloat16)
    pushed = jnp.einsum(
        "bij,cbi->cbj", mortar_part, multiplier_low, preferred_element_type=jnp.float32
    )
    condensed_low = (master_sums + pushed).astype(jnp.bfloat16)
    master_fix = jnp.einsum(
        "bkj,cbj->cbk", inverse_part, condensed_low, preferred_element_type=jnp.float32
    )
    master_low = master_fix.astype(jnp.bfloat16)
    slave_fix = (
        jnp.einsum("bij,cbj->cbi", mortar_part, master_low, preferred_element_type=jnp.float32)
        / diagonal[None]
    )
    return (slave_fix, master_fix)


def shards(contributions, send_map, arrival_map, dual_diagonal, mortar, master_inverse):
    block_count = dual_diagonal.shape[0]
    node_count = contributions.shape[3]
    comp_count = contributions.shape[1]
    row_count = contributions.shape[2]
    slot_count = send_map.shape[1]
    picked = send_map[0]
    is_live = picked >= 0
    filled = jnp.where(is_live, picked, 0)
    outgoing = jnp.take(contributions[0], filled, axis=1) * is_live[None, :, None].astype(
        jnp.float32
    )
    landing = jnp.where(is_live, picked, row_count)
    block_ids = jnp.arange(block_count, dtype=jnp.int32)
    wide_count = lax.axis_size("wide")
    half_cap = slot_count // (2 * wide_count)
    core_index = lax.axis_index("narrow")
    received_rows = lax.all_to_all(
        outgoing, ("wide", "narrow"), split_axis=1, concat_axis=1, tiled=True
    )
    received_rows = received_rows.reshape(comp_count, wide_count, 2, half_cap, node_count)
    my_arrivals = lax.dynamic_index_in_dim(
        arrival_map[0].reshape(wide_count, 2, half_cap), core_index, 1, keepdims=False
    )
    choosing_mask = (my_arrivals[:, :, None] == block_ids[None, None, :]).astype(jnp.float32)
    partial_value = jnp.einsum(
        "cosin,oib->scbn", received_rows, choosing_mask, precision=lax.Precision.HIGHEST
    )
    totals = sent_and_summed(partial_value, "narrow", 2)
    half_blocks = block_count // 2
    first_block = core_index * half_blocks
    part_diag = lax.dynamic_slice_in_dim(dual_diagonal, first_block, half_blocks, 0)
    part_mortar = lax.dynamic_slice_in_dim(mortar, first_block, half_blocks, 0)
    partition_inverse = lax.dynamic_slice_in_dim(master_inverse, first_block, half_blocks, 0)
    slave_fix, master_fix = condense(
        totals[0], totals[1], part_diag, part_mortar, partition_inverse
    )
    joined = gather_directly(jnp.stack([slave_fix, master_fix]), "narrow", 2)
    departing_rows = jnp.einsum(
        "scbn,oib->cosin", joined, choosing_mask, precision=lax.Precision.HIGHEST
    )
    departing_rows = departing_rows.reshape(comp_count, slot_count, node_count)
    returned = lax.all_to_all(
        departing_rows, ("wide", "narrow"), split_axis=1, concat_axis=1, tiled=True
    )
    placed = (
        jnp.zeros((comp_count, row_count + 1, node_count), jnp.float32)
        .at[:, landing, :]
        .set(returned)
    )
    return placed[:, :row_count][None]


def solution(mesh):
    placed = (
        P("narrow", None, "wide", None),
        P("wide", None),
        P("wide", None),
        P("wide", None),
        P("wide", None, None),
        P("wide", None, None),
    )
    return jax.shard_map(
        shards,
        mesh=mesh,
        in_specs=placed,
        out_specs=P("narrow", None, "wide", None),
        check_vma=False,
    )
```

profile of v0, /device:TPU:1, one launch (start us, length us, event | category | flops | bytes accessed | tf_op | source)
XLA Modules:
  0.0 135.7 jit_solution(10167753575181085318)
XLA Ops:
  0.0 0.0 copy-start
  0.0 0.7 fusion.36
  0.8 0.7 reduce.2
  1.5 1.7 %copy.50 = f32[1,3,512,128]{3,1,2,0:T(4,128)S(1)} copy(f32[1,3,512,128]{3,2,1,0:T(8,128)} %param.6) | data formatting | bytes 1572864 | tf_op args[0]
  3.2 3.5 %gather_fusion = f32[896,3,128]{2,1,0:T(4,128)S(1)} fusion(f32[3,512,128]{2,0,1:T(4,128)S(1)} %bitcast.79, s32[1024]{0:T(1024)S(1)} %pad_clamp_fusion), kind=kCustom, calls=%fused_computation | custom fusion | bytes 2756096 | tf_op jit(solution)/shard_map/jit(_take)/gather | solution.py:61
  6.7 5.5 %multiply_bitcast_fusion = f32[3,896,128]{2,0,1:T(4,128)} fusion(f32[896,3,128]{2,1,0:T(4,128)S(1)} %gather_fusion, f32[896]{0:T(1024)S(1)} %get-tuple-element.8, pred[896]{0:T(1024)(128)(4,1)S(1)} %get-tuple-element.7), kind=kLoop, calls=%fused_computation.8 | loop fusion | flops 688128 | bytes 2756992 | tf_op jit(solution)/shard_map/mul | solution.py:61
  12.2 0.0 copy-start.1
  12.2 11.5 %all-to-all-start = ((f32[3,896,128]{2,0,1:T(4,128)}), f32[3,896,128]{2,0,1:T(4,128)S(1)}, u32[]{:S(2)}, u32[]{:S(2)}) async-start(f32[3,896,128]{2,0,1:T(4,128)} %multiply_bitcast_fusion), calls=%async_computation | async-start | bytes 3670016 | tf_op jit(solution)/shard_map/all_to_all | solution.py:69
  23.7 0.0 copy-done.1
  23.7 0.2 reshape_squeeze.3
  24.0 0.1 copy.17
  24.1 0.0 copy-done
  24.1 27.0 %all-to-all-done = f32[3,896,128]{2,0,1:T(4,128)S(1)} async-done(((f32[3,896,128]{2,0,1:T(4,128)}), f32[3,896,128]{2,0,1:T(4,128)S(1)}, u32[]{:S(2)}, u32[]{:S(2)}) %all-to-all-start) | async-done | bytes 1376288 | tf_op jit(solution)/shard_map/all_to_all | solution.py:69
  51.1 1.1 fusion.6
  52.1 0.1 copy.51
  52.2 5.2 %all_to_all.20 = f32[2,2,3,128,128]{4,3,1,2,0:T(8,128)S(1)} all-to-all(f32[2,2,3,128,128]{4,3,1,2,0:T(8,128)S(1)} %bitcast.81), channel_id=1, replica_groups=mesh['wide'=64,'narrow'=2] {'narrow'}, dimensions={0} | all-to-all | bytes 1572864 | tf_op jit(solution)/shard_map/all_to_all | solution.py:15
  57.4 0.1 reduce_sum.9
  57.6 6.8 %fusion = f32[128,3,128]{2,1,0:T(4,128)S(1)} fusion(bf16[256,128,128]{2,1,0:T(8,128)(2,1)} %param.11, s32[]{:T(128)S(6)} %select_n.72, bf16[256,128,128]{2,1,0:T(8,128)(2,1)} %param.10, f32[1,3,128,128]{3,2,0,1:T(8,128)S(1)} %slice.14, bf16[3,128,128]{2,1,0:T(8,128)(2,1)S(1)} %fusion.32), kind=kOutput, calls=%fused_computation.2 | convolution fusion | flops 25264128 | bytes 8881152 | tf_op jit(solution)/shard_map/bkj,cbj->cbk/dot_general | solution.py:41
  64.4 4.5 %fusion.11 = f32[1,3,128,128]{3,1,2,0:T(4,128)S(1)} fusion(bf16[256,128,128]{2,1,0:T(8,128)(2,1)} %param.10, s32[]{:T(128)S(6)} %select_n.72, f32[128,128]{1,0:T(8,128)S(1)} %constant_dynamic-slice_fusion, f32[128,3,128]{2,1,0:T(4,128)S(1)} %fusion), kind=kOutput, calls=%fused_computation.13 | convolution fusion | flops 12632064 | bytes 4653060 | tf_op jit(solution)/shard_map/bij,cbj->cbi/dot_general | solution.py:46
  68.8 0.1 pad_maximum_fusion
  69.0 0.1 broadcast_in_dim.37
  69.1 4.4 %all_to_all.21 = f32[2,2,3,128,128]{4,3,2,1,0:T(8,128)S(1)} all-to-all(f32[2,2,3,128,128]{4,3,2,1,0:T(8,128)S(1)} %broadcast_in_dim.37), channel_id=1, replica_groups=mesh['wide'=64,'narrow'=2] {'narrow'}, dimensions={0} | all-to-all | bytes 1572864 | tf_op jit(solution)/shard_map/all_to_all | solution.py:21
  73.4 0.1 copy.26
  73.5 0.8 convolution_bitcast_fusion
  74.3 0.9 copy.35
  75.3 30.9 %all_to_all.22 = f32[3,896,128]{2,0,1:T(4,128)S(1)} all-to-all(f32[3,896,128]{2,0,1:T(4,128)S(1)} %bitcast.77), channel_id=1, replica_groups=mesh['wide'=64,'narrow'=2] {'wide','narrow'}, dimensions={1} | all-to-all | bytes 2752512 | tf_op jit(solution)/shard_map/all_to_all | solution.py:94
  106.2 0.1 broadcast_in_dim.32
  106.4 28.2 %scatter_fusion = f32[3,513,128]{2,0,1:T(4,128)S(1)} fusion(f32[3,513,128]{2,0,1:T(4,128)S(1)} %broadcast_in_dim.32, s32[896]{0:T(1024)S(1)} %get-tuple-element.6, f32[896,3,128]{2,1,0:T(4,128)S(1)} %bitcast.78), kind=kCustom, calls=%fused_computation.1 | custom fusion | bytes 4132352 | tf_op jit(solution)/shard_map/scatter | solution.py:100
  134.5 0.2 slice_bitcast_fusion
  134.7 0.9 copy.29
  (8 shorter events, 0.1 us)
Async XLA Ops:
  0.0 24.1 %copy-start = (f32[256,128]{1,0:T(8,128)S(1)}, f32[256,128]{1,0:T(8,128)}, u32[]{:S(2)}) copy-start(f32[256,128]{1,0:T(8,128)} %param.9) | copy-start | bytes 393220
  12.2 11.5 %copy-start.1 = (s32[1,896]{1,0:T(1,128)S(1)}, s32[1,896]{1,0:T(1,128)}, u32[]{:S(2)}) copy-start(s32[1,896]{1,0:T(1,128)} %param.8) | copy-start | bytes 10756
  12.2 38.9 %all-to-all-start = ((f32[3,896,128]{2,0,1:T(4,128)}), f32[3,896,128]{2,0,1:T(4,128)S(1)}, u32[]{:S(2)}, u32[]{:S(2)}) async-start(f32[3,896,128]{2,0,1:T(4,128)} %multiply_bitcast_fusion), calls=%async_computation | async-start | bytes 3670016 | tf_op jit(solution)/shard_map/all_to_all | solution.py:69
where the time goes:
time: 136 us
  blocking collectives  40.5 us (30%)
  local copies, waits for them, and re-layouts  36.2 us (27%)
  waiting for transfers between devices  27 us (20%)
  matrix products  13.2 us (10%)
  starting transfers between devices  11.5 us (8%)
  other arithmetic  7.16 us (5%)
    all_to_all x1, blocking collectives, shards(): lax.all_to_all(departing_rows, ('wide', 'narrow'), split_axis=1, concat_a...  30.9 us
    scatter x1, local copies, waits for them, and re-layouts, shards(): placed = jnp.zeros((comp_count, row_count + 1, node_count), jnp.float32)....  28.2 us
    all_to_all x1, waiting for transfers between devices, shards(): lax.all_to_all(outgoing, ('wide', 'narrow'), split_axis=1, concat_axis=1,...  27 us
    all_to_all x1, starting transfers between devices, shards(): lax.all_to_all(outgoing, ('wide', 'narrow'), split_axis=1, concat_axis=1,...  11.5 us
    dot_general x1, matrix products, condense(): jnp.einsum('bkj,cbj->cbk', inverse_part, condensed_low, preferred_element...  6.8 us
    mul x1, other arithmetic, shards(): jnp.take(contributions[0], filled, axis=1)  5.48 us
    all_to_all x1, blocking collectives, sent_and_summed(): lax.all_to_all(pieces, axis, split_axis=0, concat_axis=0, tiled=True)  5.25 us
    dot_general x1, matrix products, condense(): jnp.einsum('bij,cbj->cbi', mortar_part, master_low, preferred_element_typ...  4.47 us
  transfers between devices with their start and end apart: 1, of which 1 were waited for; matrix products, arithmetic and copies ran while one was open for 0% of the time, Pallas kernels for 0%

commit v1 on v0

v1 whole, which is shorter than its diff:
```python
import functools
import jax
import jax.numpy as jnp
from jax import lax
from jax.experimental import pallas as pl
from jax.experimental.pallas import tpu as pltpu
from jax.sharding import PartitionSpec as P

MESH = pl.DeviceIdType.MESH
F32 = jnp.float32
BF16 = jnp.bfloat16
N_WIDE = 64
CAP = 14
PAD = 16
ROWS = 512
BLK = 256
HALF = 128
NODES = 128
SLOTS = N_WIDE * PAD
GROUPS = ((0,), (1,), (2,))


def dot(a, b):
    return lax.dot_general(a, b, (((1,), (0,)), ((), ())), preferred_element_type=F32)


def dot_nt(a, b):
    return lax.dot_general(a, b, (((1,), (1,)), ((), ())), preferred_element_type=F32)


def split(x):
    hi = x.astype(BF16)
    lo = (x - hi.astype(F32)).astype(BF16)
    return jnp.concatenate([hi, lo], axis=1)


def padded_map(ref):
    x = jnp.concatenate([ref[:, 112 * r : 112 * (r + 1)] for r in range(8)], axis=0) + 1
    hi = (x >> 4).astype(F32).astype(BF16)
    lo = (x & 15).astype(F32).astype(BF16)
    i = lax.broadcasted_iota(jnp.int32, (112, 128), 0)
    l = lax.broadcasted_iota(jnp.int32, (112, 128), 1)
    q = jnp.where((i == (l >> 4) * CAP + (l & 15)) & ((l & 15) < CAP), 1.0, 0.0).astype(BF16)
    rows = dot(hi, q) * 16.0 + dot(lo, q) - 1.0
    cols = jnp.transpose(jnp.concatenate([rows] * 16, axis=0))
    return rows.astype(jnp.int32), cols.astype(jnp.int32)


def one_hot_cols(cols, out_ref, width):
    lane = lax.broadcasted_iota(jnp.int32, (128, width), 1)
    for r in range(8):
        out_ref[pl.ds(128 * r, 128), :] = jnp.where(cols[:, r : r + 1] == lane, 1.0, 0.0).astype(BF16)


def one_hot_rows(rows, out_ref, height):
    sub = lax.broadcasted_iota(jnp.int32, (height, 128), 0)
    for r in range(8):
        out_ref[:, pl.ds(128 * r, 128)] = jnp.where(rows[r : r + 1, :] == sub, 1.0, 0.0).astype(BF16)


def kernel(
    contrib_ref, smap_ref, amap_ref, diag_ref, mortar_hbm, inv_hbm, out_ref,
    send, recv, back, home, s_col, s_row, a_col, a_row, mortar, inverse,
    sums, other, vec, mid, fix, fixed_in,
    load_sem, send_sem, recv_sem, xs_sem, xr_sem,
):
    w = lax.axis_index("wide")
    n = lax.axis_index("narrow")
    x0, z0, y0 = w // 16, (w // 4) % 4, w % 4

    def peer(k):
        k = 64 - k
        return ((x0 + k // 16) % 4) * 16 + ((z0 + (k // 4) % 4) % 4) * 4 + (y0 + k % 4) % 4

    barrier = pltpu.get_barrier_semaphore()

    @pl.loop(1, N_WIDE)
    def _(k):
        pl.semaphore_signal(barrier, inc=1, device_id={"wide": peer(k)}, device_id_type=MESH)

    pl.semaphore_signal(barrier, inc=1, device_id={"narrow": 1 - n}, device_id_type=MESH)

    first = pl.multiple_of(n * HALF, HALF)
    load_m = pltpu.make_async_copy(mortar_hbm.at[pl.ds(first, HALF)], mortar, load_sem.at[0])
    load_i = pltpu.make_async_copy(inv_hbm.at[pl.ds(first, HALF)], inverse, load_sem.at[1])
    load_m.start()
    load_i.start()

    def exchange(src, dst, leg, c):
        @pl.loop(1, N_WIDE)
        def _(k):
            p = peer(k)
            pltpu.make_async_remote_copy(
                src_ref=src.at[c, p, pl.ds(0, CAP)],
                dst_ref=dst.at[c, w, pl.ds(0, CAP)],
                send_sem=send_sem.at[leg, c],
                recv_sem=recv_sem.at[leg, c],
                device_id={"wide": p},
                device_id_type=MESH,
            ).start()

        dst[c, pl.ds(w, 1)] = src[c, pl.ds(w, 1)]

    def all_bytes(buf, sem, c):
        ref = buf.at[c, pl.ds(0, N_WIDE - 1), pl.ds(0, CAP)]
        return pltpu.make_async_copy(ref, ref, sem)

    def swap(src, dst, leg, c):
        return pltpu.make_async_remote_copy(
            src_ref=src, dst_ref=dst, send_sem=xs_sem.at[leg, c], recv_sem=xr_sem.at[leg, c],
            device_id={"narrow": 1 - n}, device_id_type=MESH,
        )

    s_rows, s_cols = padded_map(smap_ref)
    one_hot_cols(s_cols, s_col, ROWS)
    zero = jnp.zeros((N_WIDE, PAD - CAP, NODES), F32)
    for c in range(3):
        recv[c, :, pl.ds(CAP, PAD - CAP), :] = zero
        home[c, :, pl.ds(CAP, PAD - CAP), :] = zero

    for c in range(3):
        both = dot(s_col[...], split(contrib_ref[0, c]))
        send[c] = (both[:, :NODES] + both[:, NODES:]).reshape(N_WIDE, PAD, NODES)
        if c == 0:
            pl.semaphore_wait(barrier, N_WIDE)
        exchange(send, recv, 0, c)

    one_hot_rows(s_rows, s_row, ROWS)
    a_rows, a_cols = padded_map(amap_ref)
    one_hot_rows(a_rows, a_row, BLK)
    one_hot_cols(a_cols, a_col, BLK)
    mine = pl.ds(first, HALF)
    theirs = pl.ds(pl.multiple_of((1 - n) * HALF, HALF), HALF)
    diag = diag_ref[mine, :]
    load_m.wait()
    load_i.wait()

    sub = lax.broadcasted_iota(jnp.int32, (8, NODES), 0)

    for group in GROUPS:
        for c in group:
            all_bytes(recv, recv_sem.at[0, c], c).wait()
            both = dot(a_row[...], split(recv[c].reshape(SLOTS, NODES)))
            sums[c] = both[:, :NODES] + both[:, NODES:]
            swap(sums.at[c, theirs], other.at[c], 0, c).start()
        for c in group:
            swap(sums.at[c, theirs], other.at[c], 0, c).wait()
            own = sums[c, mine, :]
            got = other[c]
            slave = jnp.where(n == 0, own, got)
            master = jnp.where(n == 0, got, own)
            vec[c] = slave / diag
            mid[c] = master

        def stage(mats, src, transposed, finish):
            @pl.loop(0, HALF // 16)
            def _(g):
                for h in range(2):
                    at = pl.ds(pl.multiple_of(g * 16 + h * 8, 8), 8)
                    parts = [src[c, at, :] for c in group]
                    acc = [jnp.zeros((8, NODES), F32)] * len(group)
                    total = None
                    for b in range(8):
                        mat = mats[g * 16 + h * 8 + b]
                        left = jnp.concatenate(
                            [jnp.where(sub == b, v, 0.0) for v in parts], axis=0
                        ).astype(BF16)
                        got = dot_nt(left, mat) if transposed else dot(left, mat)
                        total = got if total is None else total + got
                    for i, c in enumerate(group):
                        finish(c, at, total[8 * i : 8 * i + 8])

        def after_push(c, at, v):
            mid[c, at, :] = mid[c, at, :] + v

        def after_master(c, at, v):
            fix[c, 1, at, :] = v
            vec[c, at, :] = v

        def after_slave(c, at, v):
            fix[c, 0, at, :] = v / diag_ref[pl.ds(first + at.start, 8), :]

        stage(mortar, vec, False, after_push)
        stage(inverse, mid, True, after_master)
        stage(mortar, vec, True, after_slave)

        for c in group:
            swap(fix.at[c, 1 - n], fixed_in.at[c], 1, c).start()
        for c in group:
            swap(fix.at[c, 1 - n], fixed_in.at[c], 1, c).wait()
            own = fix[c, pl.ds(n, 1)][0]
            got = fixed_in[c]
            low = jnp.where(n == 0, own, got)
            high = jnp.where(n == 0, got, own)
            full = jnp.concatenate([low, high], axis=0).astype(BF16)
            back[c] = dot(a_col[...], full).reshape(N_WIDE, PAD, NODES)
            exchange(back, home, 1, c)

    for c in range(3):
        all_bytes(home, recv_sem.at[1, c], c).wait()
        out_ref[0, c] = dot(s_row[...], home[c].reshape(SLOTS, NODES).astype(BF16))

    for c in range(3):
        all_bytes(send, send_sem.at[0, c], c).wait()
        all_bytes(back, send_sem.at[1, c], c).wait()


def shards(contributions, send_map, arrival_map, dual_diagonal, mortar, master_inverse):
    vmem = pl.BlockSpec(memory_space=pltpu.VMEM)
    hbm = pl.BlockSpec(memory_space=pl.ANY)
    packets = pltpu.VMEM((3, N_WIDE, PAD, NODES), F32)
    return pl.pallas_call(
        kernel,
        out_shape=jax.ShapeDtypeStruct(contributions.shape, F32),
        in_specs=[vmem, vmem, vmem, vmem, hbm, hbm],
        out_specs=vmem,
        scratch_shapes=[
            packets, packets, packets, packets,
            pltpu.VMEM((SLOTS, ROWS), BF16),
            pltpu.VMEM((ROWS, SLOTS), BF16),
            pltpu.VMEM((SLOTS, BLK), BF16),
            pltpu.VMEM((BLK, SLOTS), BF16),
            pltpu.VMEM((HALF, NODES, NODES), BF16),
            pltpu.VMEM((HALF, NODES, NODES), BF16),
            pltpu.VMEM((3, BLK, NODES), F32),
            pltpu.VMEM((3, HALF, NODES), F32),
            pltpu.VMEM((3, HALF, NODES), F32),
            pltpu.VMEM((3, HALF, NODES), F32),
            pltpu.VMEM((3, 2, HALF, NODES), F32),
            pltpu.VMEM((3, HALF, NODES), F32),
            pltpu.SemaphoreType.DMA((2,)),
            pltpu.SemaphoreType.DMA((2, 3)),
            pltpu.SemaphoreType.DMA((2, 3)),
            pltpu.SemaphoreType.DMA((2, 3)),
            pltpu.SemaphoreType.DMA((2, 3)),
        ],
        compiler_params=pltpu.CompilerParams(
            collective_id=0, has_side_effects=True, vmem_limit_bytes=56 * 1024 * 1024
        ),
        name="mortar",
    )(contributions, send_map, arrival_map, dual_diagonal, mortar, master_inverse)


def solution(mesh):
    placed = (
        P("narrow", None, "wide", None),
        P("wide", None),
        P("wide", None),
        P("wide", None),
        P("wide", None, None),
        P("wide", None, None),
    )
    return jax.shard_map(
        shards,
        mesh=mesh,
        in_specs=placed,
        out_specs=P("narrow", None, "wide", None),
        check_vma=False,
    )
```

time: 136 us -> 78.3 us (0.58)
  Pallas kernels: 0 us -> 76.1 us
  blocking collectives: 40.5 us -> 0 us
  local copies, waits for them, and re-layouts: 36.2 us -> 2.06 us
  waiting for transfers between devices: 27 us -> 0 us
  matrix products: 13.2 us -> 0 us
  starting transfers between devices: 11.5 us -> 0 us
  other arithmetic: 7.16 us -> 0 us
    pallas_call x0 -> x1, Pallas kernels: none -> 76.1 us  [shards(): pl.pallas_call(kernel, out_shape=jax.ShapeDtypeStruct(contributions.shape...]
    all_to_all x3 -> x0, blocking collectives: 40.5 us -> none  [the longest x1 30.9 us: shards(): lax.all_to_all(departing_rows, ('wide', 'narrow'), split_axis=1, concat_a...]
    scatter x1 -> x0, local copies, waits for them, and re-layouts: 28.2 us -> none  [shards(): placed = jnp.zeros((comp_count, row_count + 1, node_count), jnp.float32)....]
    all_to_all x1 -> x0, waiting for transfers between devices: 27 us -> none  [shards(): lax.all_to_all(outgoing, ('wide', 'narrow'), split_axis=1, concat_axis=1,...]
    dot_general x4 -> x0, matrix products: 13.2 us -> none  [the longest x1 6.8 us: condense(): jnp.einsum('bkj,cbj->cbk', inverse_part, condensed_low, preferred_element...]
    all_to_all x1 -> x0, starting transfers between devices: 11.5 us -> none  [shards(): lax.all_to_all(outgoing, ('wide', 'narrow'), split_axis=1, concat_axis=1,...]
    mul x1 -> x0, other arithmetic: 5.48 us -> none  [shards(): jnp.take(contributions[0], filled, axis=1)]
    gather x1 -> x0, local copies, waits for them, and re-layouts: 3.53 us -> none  [shards(): jnp.take(contributions[0], filled, axis=1)]
  transfers between devices with their start and end apart: 1 -> 0, of which waited for: 1 -> 0; matrix products, arithmetic and copies ran while one was open for 0% -> 0% of each run, Pallas kernels for 0% -> 0%
where the time goes in v1:
time: 78.3 us; the launch traced here: 78.2 us
  Pallas kernels  76.1 us (97%)
  local copies, waits for them, and re-layouts  2.06 us (3%)
    pallas_call x1, Pallas kernels, shards(): pl.pallas_call(kernel, out_shape=jax.ShapeDtypeStruct(contributions.shape...  76.1 us
    unnamed x1, local copies, waits for them, and re-layouts  2.06 us

profile of v1, /device:TPU:1, one launch (start us, length us, event | category | flops | bytes accessed | tf_op | source)
XLA Modules:
  0.0 78.2 jit_solution(11203454970845595045)
XLA Ops:
  0.0 76.1 %mortar.1 = f32[1,3,512,128]{3,2,1,0:T(8,128)} custom-call(f32[1,3,512,128]{3,2,1,0:T(8,128)} %contrib_ref.1, s32[1,896]{1,0:T(1,128)} %smap_ref.1, s32[1,896]{1,0:T(1,128)} %amap_ref.1, f32[256,128]{1,0:T(8,128)} %diag_ref.1, bf16[256,128,128]{2,1,0:T(8,128)(2,1)} %mortar_hbm.1, bf16[256,128,128]{2,1,0:T(8,128)(2,1)} %inv_hbm.1), custom_call_target="tpu_custom_call" | custom-call | tf_op jit(solution)/shard_map/mortar/pallas_call | solution.py:212
  76.1 2.1 %copy.8 = f32[1,3,512,128]{3,2,1,0:T(8,128)} copy(f32[1,3,512,128]{3,2,1,0:T(8,128)} %mortar.1) | data formatting | bytes 1572864

commit v2 on v1

v2 whole, which is shorter than its diff:
```python
import functools
import jax
import jax.numpy as jnp
from jax import lax
from jax.experimental import pallas as pl
from jax.experimental.pallas import tpu as pltpu
from jax.sharding import PartitionSpec as P

MESH = pl.DeviceIdType.MESH
F32 = jnp.float32
BF16 = jnp.bfloat16
N_WIDE = 64
CAP = 14
PAD = 16
ROWS = 512
BLK = 256
HALF = 128
NODES = 128
SLOTS = N_WIDE * PAD
CHUNK = 128


def hops(o):
    return sum(min(v, 4 - v) for v in o)


OFFSETS = sorted(
    ((i // 16, (i // 4) % 4, i % 4) for i in range(1, N_WIDE)),
    key=lambda o: (-hops(o), (o[0] * 5 + o[1] * 3 + o[2] * 7) % 11),
)


def dot(a, b):
    return lax.dot_general(a, b, (((1,), (0,)), ((), ())), preferred_element_type=F32)


def dot_nt(a, b):
    return lax.dot_general(a, b, (((1,), (1,)), ((), ())), preferred_element_type=F32)


def split(x):
    hi = x.astype(BF16)
    lo = (x - hi.astype(F32)).astype(BF16)
    return jnp.concatenate([hi, lo], axis=1)


def padded_map(ref):
    x = jnp.concatenate([ref[:, 112 * r : 112 * (r + 1)] for r in range(8)], axis=0) + 1
    hi = (x >> 4).astype(F32).astype(BF16)
    lo = (x & 15).astype(F32).astype(BF16)
    i = lax.broadcasted_iota(jnp.int32, (112, 128), 0)
    l = lax.broadcasted_iota(jnp.int32, (112, 128), 1)
    q = jnp.where((i == (l >> 4) * CAP + (l & 15)) & ((l & 15) < CAP), 1.0, 0.0).astype(BF16)
    rows = dot(hi, q) * 16.0 + dot(lo, q) - 1.0
    cols = jnp.transpose(jnp.concatenate([rows] * 16, axis=0))
    return rows.astype(jnp.int32), cols.astype(jnp.int32)


def one_hot_cols(cols, out_ref, width):
    lane = lax.broadcasted_iota(jnp.int32, (128, width), 1)
    for r in range(8):
        out_ref[pl.ds(128 * r, 128), :] = jnp.where(cols[:, r : r + 1] == lane, 1.0, 0.0).astype(BF16)


def one_hot_rows(rows, out_ref, height):
    sub = lax.broadcasted_iota(jnp.int32, (height, 128), 0)
    for r in range(8):
        out_ref[:, pl.ds(128 * r, 128)] = jnp.where(rows[r : r + 1, :] == sub, 1.0, 0.0).astype(BF16)


def kernel(
    contrib_hbm, smap_hbm, amap_hbm, diag_hbm, mortar_hbm, inv_hbm, out_ref,
    contrib, smap, amap, diag, send, recv, back, home,
    s_col, s_row, a_col, a_row, mortar, mortar_t, inverse,
    sums, other, vec, mid, fix, fixed_in,
    load_sem, send_sem, recv_sem, xs_sem, xr_sem,
):
    w = lax.axis_index("wide")
    n = lax.axis_index("narrow")
    x0, z0, y0 = w // 16, (w // 4) % 4, w % 4
    xs = [(x0 + i) % 4 * 16 for i in range(4)]
    zs = [(z0 + i) % 4 * 4 for i in range(4)]
    ys = [(y0 + i) % 4 for i in range(4)]
    peers = [xs[i] + zs[j] + ys[k] for i, j, k in OFFSETS]

    barrier = pltpu.get_barrier_semaphore()
    for p in peers:
        pl.semaphore_signal(barrier, inc=1, device_id={"wide": p}, device_id_type=MESH)
    pl.semaphore_signal(barrier, inc=1, device_id={"narrow": 1 - n}, device_id_type=MESH)

    first = pl.multiple_of(n * HALF, HALF)
    mine = pl.ds(first, HALF)
    second = pl.multiple_of((1 - n) * HALF, HALF)
    theirs = pl.ds(second, HALF)
    loads = [
        pltpu.make_async_copy(src, dst, load_sem.at[i])
        for i, (src, dst) in enumerate(
            [
                (smap_hbm, smap),
                (contrib_hbm.at[0], contrib),
                (amap_hbm, amap),
                (diag_hbm.at[mine], diag),
                (mortar_hbm.at[mine], mortar),
                (inv_hbm.at[mine], inverse),
            ]
        )
    ]
    for load in loads:
        load.start()

    def exchange(src, dst, leg, c):
        for p in peers:
            pltpu.make_async_remote_copy(
                src_ref=src.at[c, p, pl.ds(0, CAP)],
                dst_ref=dst.at[c, w, pl.ds(0, CAP)],
                send_sem=send_sem.at[leg, c],
                recv_sem=recv_sem.at[leg, c],
                device_id={"wide": p},
                device_id_type=MESH,
            ).start()
        dst[c, pl.ds(w, 1)] = src[c, pl.ds(w, 1)]

    def all_bytes(buf, sem, c):
        ref = buf.at[c, pl.ds(0, N_WIDE - 1), pl.ds(0, CAP)]
        return pltpu.make_async_copy(ref, ref, sem)

    def swap(src, dst, leg, c):
        return pltpu.make_async_remote_copy(
            src_ref=src, dst_ref=dst, send_sem=xs_sem.at[leg, c], recv_sem=xr_sem.at[leg, c],
            device_id={"narrow": 1 - n}, device_id_type=MESH,
        )

    loads[0].wait()
    s_rows, s_cols = padded_map(smap)
    one_hot_cols(s_cols, s_col, ROWS)
    zero = jnp.zeros((N_WIDE, PAD - CAP, NODES), F32)
    for c in range(3):
        recv[c, :, pl.ds(CAP, PAD - CAP), :] = zero
        home[c, :, pl.ds(CAP, PAD - CAP), :] = zero
    loads[1].wait()

    for c in range(3):
        both = dot(s_col[...], split(contrib[c]))
        send[c] = (both[:, :NODES] + both[:, NODES:]).reshape(N_WIDE, PAD, NODES)
        if c == 0:
            pl.semaphore_wait(barrier, N_WIDE)
        exchange(send, recv, 0, c)

    for load in loads[2:]:
        load.wait()
    a_rows, a_cols = padded_map(amap)
    one_hot_rows(a_rows, a_row, BLK)
    one_hot_cols(a_cols, a_col, BLK)
    eye = jnp.where(
        lax.broadcasted_iota(jnp.int32, (NODES, NODES), 0)
        == lax.broadcasted_iota(jnp.int32, (NODES, NODES), 1),
        1.0,
        0.0,
    ).astype(BF16)

    @pl.loop(0, HALF // 8)
    def _(g):
        for b in range(8):
            inverse[g * 8 + b] = dot_nt(eye, inverse[g * 8 + b]).astype(BF16)
            mortar_t[g * 8 + b] = dot_nt(eye, mortar[g * 8 + b]).astype(BF16)

    one_hot_rows(s_rows, s_row, ROWS)
    sub = lax.broadcasted_iota(jnp.int32, (8, NODES), 0)

    def block_sums(c):
        all_bytes(recv, recv_sem.at[0, c], c).wait()
        both_in = split(recv[c].reshape(SLOTS, NODES))
        both = dot(a_row[theirs, :], both_in)
        sums[c, theirs, :] = both[:, :NODES] + both[:, NODES:]
        swap(sums.at[c, theirs], other.at[c], 0, c).start()
        both = dot(a_row[mine, :], both_in)
        sums[c, mine, :] = both[:, :NODES] + both[:, NODES:]

    def stage(mats, src, finish):
        @pl.loop(0, HALF // CHUNK)
        def _(g):
            for h in range(CHUNK // 8):
                at = pl.ds(pl.multiple_of(g * CHUNK + h * 8, 8), 8)
                v = src[at, :]
                total = None
                for b in range(8):
                    left = jnp.where(sub == b, v, 0.0).astype(BF16)
                    got = dot(left, mats[g * CHUNK + h * 8 + b])
                    total = got if total is None else total + got
                finish(at, total)

    def solve(c):
        swap(sums.at[c, theirs], other.at[c], 0, c).wait()
        own = sums[c, mine, :]
        got = other[c]
        vec[c] = jnp.where(n == 0, own, got) / diag[...]
        mid[c] = jnp.where(n == 0, got, own)

        def after_push(at, v):
            mid[c, at, :] = mid[c, at, :] + v

        def after_master(at, v):
            fix[c, 1, at, :] = v

        def after_slave(at, v):
            fix[c, 0, at, :] = v / diag[at, :]

        stage(mortar, vec.at[c], after_push)
        stage(inverse, mid.at[c], after_master)
        stage(mortar_t, fix.at[c, 1], after_slave)
        swap(fix.at[c, 1 - n], fixed_in.at[c], 1, c).start()

    def give_back(c):
        own = fix[c, pl.ds(n, 1)][0]
        swap(fix.at[c, 1 - n], fixed_in.at[c], 1, c).wait()
        got = fixed_in[c]
        low = jnp.where(n == 0, own, got)
        high = jnp.where(n == 0, got, own)
        full = jnp.concatenate([low, high], axis=0).astype(BF16)
        back[c] = dot(a_col[...], full).reshape(N_WIDE, PAD, NODES)
        exchange(back, home, 1, c)

    block_sums(0)
    solve(0)
    block_sums(1)
    give_back(0)
    solve(1)
    block_sums(2)
    give_back(1)
    solve(2)
    give_back(2)

    for c in range(3):
        all_bytes(home, recv_sem.at[1, c], c).wait()
        out_ref[0, c] = dot(s_row[...], home[c].reshape(SLOTS, NODES).astype(BF16))

    for c in range(3):
        all_bytes(send, send_sem.at[0, c], c).wait()
        all_bytes(back, send_sem.at[1, c], c).wait()


def shards(contributions, send_map, arrival_map, dual_diagonal, mortar, master_inverse):
    vmem = pl.BlockSpec(memory_space=pltpu.VMEM)
    hbm = pl.BlockSpec(memory_space=pltpu.HBM)
    packets = pltpu.VMEM((3, N_WIDE, PAD, NODES), F32)
    return pl.pallas_call(
        kernel,
        out_shape=jax.ShapeDtypeStruct(contributions.shape, F32),
        in_specs=[hbm] * 6,
        out_specs=vmem,
        scratch_shapes=[
            pltpu.VMEM((3, ROWS, NODES), F32),
            pltpu.VMEM((1, N_WIDE * CAP), jnp.int32),
            pltpu.VMEM((1, N_WIDE * CAP), jnp.int32),
            pltpu.VMEM((HALF, NODES), F32),
            packets, packets, packets, packets,
            pltpu.VMEM((SLOTS, ROWS), BF16),
            pltpu.VMEM((ROWS, SLOTS), BF16),
            pltpu.VMEM((SLOTS, BLK), BF16),
            pltpu.VMEM((BLK, SLOTS), BF16),
            pltpu.VMEM((HALF, NODES, NODES), BF16),
            pltpu.VMEM((HALF, NODES, NODES), BF16),
            pltpu.VMEM((HALF, NODES, NODES), BF16),
            pltpu.VMEM((3, BLK, NODES), F32),
            pltpu.VMEM((3, HALF, NODES), F32),
            pltpu.VMEM((3, HALF, NODES), F32),
            pltpu.VMEM((3, HALF, NODES), F32),
            pltpu.VMEM((3, 2, HALF, NODES), F32),
            pltpu.VMEM((3, HALF, NODES), F32),
            pltpu.SemaphoreType.DMA((6,)),
            pltpu.SemaphoreType.DMA((2, 3)),
            pltpu.SemaphoreType.DMA((2, 3)),
            pltpu.SemaphoreType.DMA((2, 3)),
            pltpu.SemaphoreType.DMA((2, 3)),
        ],
        compiler_params=pltpu.CompilerParams(
            collective_id=0, has_side_effects=True, vmem_limit_bytes=40 * 1024 * 1024
        ),
        name="mortar",
    )(*(pltpu.with_memory_space_constraint(v, pltpu.HBM) for v in (contributions, send_map, arrival_map, dual_diagonal, mortar, master_inverse)))


def solution(mesh):
    placed = (
        P("narrow", None, "wide", None),
        P("wide", None),
        P("wide", None),
        P("wide", None),
        P("wide", None, None),
        P("wide", None, None),
    )
    return jax.shard_map(
        shards,
        mesh=mesh,
        in_specs=placed,
        out_specs=P("narrow", None, "wide", None),
        check_vma=False,
    )
```

time: 78.3 us -> 47.9 us (0.61)
  Pallas kernels: 76.1 us -> 46.9 us
  local copies, waits for them, and re-layouts: 2.06 us -> 0.88 us
    pallas_call x1, Pallas kernels: 76.1 us -> 46.9 us  [shards(): pl.pallas_call(kernel, out_shape=jax.ShapeDtypeStruct(contributions.shape...]
    unnamed x1, local copies, waits for them, and re-layouts: 2.06 us -> 0.88 us
where the time goes in v2:
time: 47.9 us; the launch traced here: 47.8 us
  Pallas kernels  46.9 us (98%)
  local copies, waits for them, and re-layouts  0.88 us (2%)
    pallas_call x1, Pallas kernels, shards(): pl.pallas_call(kernel, out_shape=jax.ShapeDtypeStruct(contributions.shape...  46.9 us

profile of v2, /device:TPU:1, one launch (start us, length us, event | category | flops | bytes accessed | tf_op | source)
XLA Modules:
  0.0 47.8 jit_solution(16536081272447504335)
XLA Ops:
  0.0 46.9 %mortar.1 = f32[1,3,512,128]{3,2,1,0:T(8,128)S(1)} custom-call(f32[1,3,512,128]{3,2,1,0:T(8,128)} %contrib_hbm.1, s32[1,896]{1,0:T(1,128)} %smap_hbm.1, s32[1,896]{1,0:T(1,128)} %amap_hbm.1, f32[256,128]{1,0:T(8,128)} %diag_hbm.1, bf16[256,128,128]{2,1,0:T(8,128)(2,1)} %mortar_hbm.1, bf16[256,128,128]{2,1,0:T(8,128)(2,1)} %inv_hbm.1), custom_call_target="tpu_custom_call" | custom-call | tf_op jit(solution)/shard_map/mortar/pallas_call | solution.py:246
  46.9 0.9 %copy.8 = f32[1,3,512,128]{3,2,1,0:T(8,128)} copy(f32[1,3,512,128]{3,2,1,0:T(8,128)S(1)} %mortar.1) | data formatting | bytes 1572864

commit v3 on v2

--- a/solution.py
+++ b/solution.py
@@ -18,6 +18,7 @@
 NODES = 128
 SLOTS = N_WIDE * PAD
 CHUNK = 128
+TURN = 16
 
 
 def hops(o):
@@ -82,11 +83,6 @@
     zs = [(z0 + i) % 4 * 4 for i in range(4)]
     ys = [(y0 + i) % 4 for i in range(4)]
     peers = [xs[i] + zs[j] + ys[k] for i, j, k in OFFSETS]
-
-    barrier = pltpu.get_barrier_semaphore()
-    for p in peers:
-        pl.semaphore_signal(barrier, inc=1, device_id={"wide": p}, device_id_type=MESH)
-    pl.semaphore_signal(barrier, inc=1, device_id={"narrow": 1 - n}, device_id_type=MESH)
 
     first = pl.multiple_of(n * HALF, HALF)
     mine = pl.ds(first, HALF)
@@ -108,6 +104,11 @@
     for load in loads:
         load.start()
 
+    barrier = pltpu.get_barrier_semaphore()
+    for p in peers:
+        pl.semaphore_signal(barrier, inc=1, device_id={"wide": p}, device_id_type=MESH)
+    pl.semaphore_signal(barrier, inc=1, device_id={"narrow": 1 - n}, device_id_type=MESH)
+
     def exchange(src, dst, leg, c):
         for p in peers:
             pltpu.make_async_remote_copy(
@@ -139,42 +140,39 @@
         home[c, :, pl.ds(CAP, PAD - CAP), :] = zero
     loads[1].wait()
 
-    for c in range(3):
+    def gather(c):
         both = dot(s_col[...], split(contrib[c]))
         send[c] = (both[:, :NODES] + both[:, NODES:]).reshape(N_WIDE, PAD, NODES)
-        if c == 0:
-            pl.semaphore_wait(barrier, N_WIDE)
-        exchange(send, recv, 0, c)
-
-    for load in loads[2:]:
-        load.wait()
+
+    def turn(src, dst, lo, hi):
+        @pl.loop(lo // TURN, hi // TURN)
+        def _(g):
+            for b in range(TURN):
+                dst[g * TURN + b] = jnp.transpose(src[g * TURN + b])
+
+    gather(0)
+    pl.semaphore_wait(barrier, N_WIDE)
+    exchange(send, recv, 0, 0)
+    gather(1)
+    loads[5].wait()
+    turn(inverse, inverse, 0, HALF)
+    loads[4].wait()
+    turn(mortar, mortar_t, 0, HALF)
+    all_bytes(send, send_sem.at[0, 0], 0).wait()
+    exchange(send, recv, 0, 1)
+    gather(2)
+    loads[2].wait()
+    loads[3].wait()
     a_rows, a_cols = padded_map(amap)
     one_hot_rows(a_rows, a_row, BLK)
-    one_hot_cols(a_cols, a_col, BLK)
-    eye = jnp.where(
-        lax.broadcasted_iota(jnp.int32, (NODES, NODES), 0)
-        == lax.broadcasted_iota(jnp.int32, (NODES, NODES), 1),
-        1.0,
-        0.0,
-    ).astype(BF16)
-
-    @pl.loop(0, HALF // 8)
-    def _(g):
-        for b in range(8):
-            inverse[g * 8 + b] = dot_nt(eye, inverse[g * 8 + b]).astype(BF16)
-            mortar_t[g * 8 + b] = dot_nt(eye, mortar[g * 8 + b]).astype(BF16)
-
-    one_hot_rows(s_rows, s_row, ROWS)
     sub = lax.broadcasted_iota(jnp.int32, (8, NODES), 0)
 
     def block_sums(c):
         all_bytes(recv, recv_sem.at[0, c], c).wait()
         both_in = split(recv[c].reshape(SLOTS, NODES))
-        both = dot(a_row[theirs, :], both_in)
-        sums[c, theirs, :] = both[:, :NODES] + both[:, NODES:]
+        both = dot(a_row[...], both_in)
+        sums[c] = both[:, :NODES] + both[:, NODES:]
         swap(sums.at[c, theirs], other.at[c], 0, c).start()
-        both = dot(a_row[mine, :], both_in)
-        sums[c, mine, :] = both[:, :NODES] + both[:, NODES:]
 
     def stage(mats, src, finish):
         @pl.loop(0, HALF // CHUNK)
@@ -220,22 +218,29 @@
         back[c] = dot(a_col[...], full).reshape(N_WIDE, PAD, NODES)
         exchange(back, home, 1, c)
 
+    def place(c):
+        all_bytes(home, recv_sem.at[1, c], c).wait()
+        out_ref[0, c] = dot(s_row[...], home[c].reshape(SLOTS, NODES).astype(BF16))
+
     block_sums(0)
+    exchange(send, recv, 0, 2)
+    one_hot_cols(a_cols, a_col, BLK)
     solve(0)
     block_sums(1)
+    one_hot_rows(s_rows, s_row, ROWS)
     give_back(0)
     solve(1)
     block_sums(2)
     give_back(1)
     solve(2)
+    place(0)
     give_back(2)
+    place(1)
+    place(2)
 
     for c in range(3):
-        all_bytes(home, recv_sem.at[1, c], c).wait()
-        out_ref[0, c] = dot(s_row[...], home[c].reshape(SLOTS, NODES).astype(BF16))
-
-    for c in range(3):
-        all_bytes(send, send_sem.at[0, c], c).wait()
+        if c:
+            all_bytes(send, send_sem.at[0, c], c).wait()
         all_bytes(back, send_sem.at[1, c], c).wait()
 
 

time: 47.9 us -> 47.1 us (0.983)
  Pallas kernels: 46.9 us -> 46.2 us
    pallas_call x1, Pallas kernels: 46.9 us -> 46.2 us  [shards(): pl.pallas_call(kernel, out_shape=jax.ShapeDtypeStruct(contributions.shape...]
where the time goes in v3:
time: 47.1 us; the launch traced here: 47 us
  Pallas kernels  46.2 us (98%)
  local copies, waits for them, and re-layouts  0.88 us (2%)
    pallas_call x1, Pallas kernels, shards(): pl.pallas_call(kernel, out_shape=jax.ShapeDtypeStruct(contributions.shape...  46.2 us

profile of v3, /device:TPU:1, one launch (start us, length us, event | category | flops | bytes accessed | tf_op | source)
XLA Modules:
  0.0 47.0 jit_solution(5413475527643899409)
XLA Ops:
  0.0 46.2 %mortar.1 = f32[1,3,512,128]{3,2,1,0:T(8,128)S(1)} custom-call(f32[1,3,512,128]{3,2,1,0:T(8,128)} %contrib_hbm.1, s32[1,896]{1,0:T(1,128)} %smap_hbm.1, s32[1,896]{1,0:T(1,128)} %amap_hbm.1, f32[256,128]{1,0:T(8,128)} %diag_hbm.1, bf16[256,128,128]{2,1,0:T(8,128)(2,1)} %mortar_hbm.1, bf16[256,128,128]{2,1,0:T(8,128)(2,1)} %inv_hbm.1), custom_call_target="tpu_custom_call" | custom-call | tf_op jit(solution)/shard_map/mortar/pallas_call | solution.py:251
  46.2 0.9 %copy.8 = f32[1,3,512,128]{3,2,1,0:T(8,128)} copy(f32[1,3,512,128]{3,2,1,0:T(8,128)S(1)} %mortar.1) | data formatting | bytes 1572864

commit v4 on v3

--- a/solution.py
+++ b/solution.py
@@ -21,14 +21,18 @@
 TURN = 16
 
 
-def hops(o):
-    return sum(min(v, 4 - v) for v in o)
-
-
-OFFSETS = sorted(
-    ((i // 16, (i // 4) % 4, i % 4) for i in range(1, N_WIDE)),
-    key=lambda o: (-hops(o), (o[0] * 5 + o[1] * 3 + o[2] * 7) % 11),
-)
+OUT = [
+    42, 26, 58, 38, 46, 43, 41, 37, 39, 59, 47, 54, 30, 62, 27, 40,
+    25, 45, 22, 57, 34, 10, 44, 55, 50, 18, 23, 36, 24, 61, 9, 29,
+    35, 14, 56, 6, 31, 11, 63, 33, 53, 21, 19, 49, 7, 17, 5, 52,
+    28, 15, 32, 2, 20, 51, 60, 13, 8, 4, 1, 16, 12, 3, 48,
+]
+BACK = [
+    42, 46, 41, 58, 26, 43, 38, 22, 39, 34, 45, 40, 62, 30, 57, 25,
+    47, 10, 37, 59, 27, 54, 24, 14, 63, 9, 31, 36, 53, 21, 11, 6,
+    33, 55, 23, 50, 18, 44, 35, 61, 29, 56, 49, 17, 7, 60, 2, 28,
+    51, 19, 13, 8, 52, 15, 20, 5, 32, 4, 48, 16, 1, 12, 3,
+]
 
 
 def dot(a, b):
@@ -82,7 +86,9 @@
     xs = [(x0 + i) % 4 * 16 for i in range(4)]
     zs = [(z0 + i) % 4 * 4 for i in range(4)]
     ys = [(y0 + i) % 4 for i in range(4)]
-    peers = [xs[i] + zs[j] + ys[k] for i, j, k in OFFSETS]
+    peers, peers_back = (
+        [xs[v // 16] + zs[(v // 4) % 4] + ys[v % 4] for v in order] for order in (OUT, BACK)
+    )
 
     first = pl.multiple_of(n * HALF, HALF)
     mine = pl.ds(first, HALF)
@@ -110,7 +116,7 @@
     pl.semaphore_signal(barrier, inc=1, device_id={"narrow": 1 - n}, device_id_type=MESH)
 
     def exchange(src, dst, leg, c):
-        for p in peers:
+        for p in (peers, peers_back)[leg]:
             pltpu.make_async_remote_copy(
                 src_ref=src.at[c, p, pl.ds(0, CAP)],
                 dst_ref=dst.at[c, w, pl.ds(0, CAP)],
@@ -158,7 +164,6 @@
     turn(inverse, inverse, 0, HALF)
     loads[4].wait()
     turn(mortar, mortar_t, 0, HALF)
-    all_bytes(send, send_sem.at[0, 0], 0).wait()
     exchange(send, recv, 0, 1)
     gather(2)
     loads[2].wait()
@@ -226,8 +231,8 @@
     exchange(send, recv, 0, 2)
     one_hot_cols(a_cols, a_col, BLK)
     solve(0)
+    one_hot_rows(s_rows, s_row, ROWS)
     block_sums(1)
-    one_hot_rows(s_rows, s_row, ROWS)
     give_back(0)
     solve(1)
     block_sums(2)
@@ -239,8 +244,7 @@
     place(2)
 
     for c in range(3):
-        if c:
-            all_bytes(send, send_sem.at[0, c], c).wait()
+        all_bytes(send, send_sem.at[0, c], c).wait()
         all_bytes(back, send_sem.at[1, c], c).wait()
 
 

time: 47.1 us -> 46.7 us (level)
  Pallas kernels: 46.2 us -> 45.7 us
where the time goes in v4:
time: 46.7 us; the launch traced here: 46.6 us
  Pallas kernels  45.7 us (98%)
  local copies, waits for them, and re-layouts  0.88 us (2%)
    pallas_call x1, Pallas kernels, shards(): pl.pallas_call(kernel, out_shape=jax.ShapeDtypeStruct(contributions.shape...  45.7 us

profile of v4, /device:TPU:1, one launch (start us, length us, event | category | flops | bytes accessed | tf_op | source)
XLA Modules:
  0.0 46.6 jit_solution(17856416129797878880)
XLA Ops:
  0.0 45.7 %mortar.1 = f32[1,3,512,128]{3,2,1,0:T(8,128)S(1)} custom-call(f32[1,3,512,128]{3,2,1,0:T(8,128)} %contrib_hbm.1, s32[1,896]{1,0:T(1,128)} %smap_hbm.1, s32[1,896]{1,0:T(1,128)} %amap_hbm.1, f32[256,128]{1,0:T(8,128)} %diag_hbm.1, bf16[256,128,128]{2,1,0:T(8,128)(2,1)} %mortar_hbm.1, bf16[256,128,128]{2,1,0:T(8,128)(2,1)} %inv_hbm.1), custom_call_target="tpu_custom_call" | custom-call | tf_op jit(solution)/shard_map/mortar/pallas_call | solution.py:255
  45.7 0.9 %copy.8 = f32[1,3,512,128]{3,2,1,0:T(8,128)} copy(f32[1,3,512,128]{3,2,1,0:T(8,128)S(1)} %mortar.1) | data formatting | bytes 1572864

commit v5 on v4

--- a/solution.py
+++ b/solution.py
@@ -164,8 +164,8 @@
     turn(inverse, inverse, 0, HALF)
     loads[4].wait()
     turn(mortar, mortar_t, 0, HALF)
+    gather(2)
     exchange(send, recv, 0, 1)
-    gather(2)
     loads[2].wait()
     loads[3].wait()
     a_rows, a_cols = padded_map(amap)
@@ -225,7 +225,7 @@
 
     def place(c):
         all_bytes(home, recv_sem.at[1, c], c).wait()
-        out_ref[0, c] = dot(s_row[...], home[c].reshape(SLOTS, NODES).astype(BF16))
+        out_ref[0, c] = dot(s_row[...], home[c].reshape(SLOTS, NODES).astype(BF16)).astype(BF16)
 
     block_sums(0)
     exchange(send, recv, 0, 2)
@@ -254,7 +254,7 @@
     packets = pltpu.VMEM((3, N_WIDE, PAD, NODES), F32)
     return pl.pallas_call(
         kernel,
-        out_shape=jax.ShapeDtypeStruct(contributions.shape, F32),
+        out_shape=jax.ShapeDtypeStruct(contributions.shape, BF16),
         in_specs=[hbm] * 6,
         out_specs=vmem,
         scratch_shapes=[
@@ -286,7 +286,7 @@
             collective_id=0, has_side_effects=True, vmem_limit_bytes=40 * 1024 * 1024
         ),
         name="mortar",
-    )(*(pltpu.with_memory_space_constraint(v, pltpu.HBM) for v in (contributions, send_map, arrival_map, dual_diagonal, mortar, master_inverse)))
+    )(*(pltpu.with_memory_space_constraint(v, pltpu.HBM) for v in (contributions, send_map, arrival_map, dual_diagonal, mortar, master_inverse))).astype(F32)
 
 
 def solution(mesh):

time: 46.7 us -> 46.7 us (level)
  other arithmetic: 0 us -> 0.93 us
  local copies, waits for them, and re-layouts: 0.88 us -> 0 us
    convert_element_type x0 -> x1, other arithmetic: none -> 0.93 us  [shards(): return pl.pallas_call(kernel, out_shape=jax.ShapeDtypeStruct(contribution...]
    unnamed x1 -> x0, local copies, waits for them, and re-layouts: 0.88 us -> none
where the time goes in v5:
time: 46.7 us; the launch traced here: 46.3 us
  Pallas kernels  45.4 us (97%)
  other arithmetic  0.93 us (2%)
    pallas_call x1, Pallas kernels, shards(): pl.pallas_call(kernel, out_shape=jax.ShapeDtypeStruct(contributions.shape...  45.4 us

profile of v5, /device:TPU:1, one launch (start us, length us, event | category | flops | bytes accessed | tf_op | source)
XLA Modules:
  0.0 46.3 jit_solution(16079391310981890743)
XLA Ops:
  0.0 45.4 %mortar.1 = bf16[1,3,512,128]{3,2,1,0:T(8,128)(2,1)S(1)} custom-call(f32[1,3,512,128]{3,2,1,0:T(8,128)} %contrib_hbm.1, s32[1,896]{1,0:T(1,128)} %smap_hbm.1, s32[1,896]{1,0:T(1,128)} %amap_hbm.1, f32[256,128]{1,0:T(8,128)} %diag_hbm.1, bf16[256,128,128]{2,1,0:T(8,128)(2,1)} %mortar_hbm.1, bf16[256,128,128]{2,1,0:T(8,128)(2,1)} %inv_hbm.1), custom_call_target="tpu_custom_call" | custom-call | tf_op jit(solution)/shard_map/mortar/pallas_call | solution.py:255
  45.4 0.9 %convert_element_type.3 = f32[1,3,512,128]{3,2,1,0:T(8,128)} convert(bf16[1,3,512,128]{3,2,1,0:T(8,128)(2,1)S(1)} %mortar.1) | non-fusion elementwise | flops 196608 | bytes 1179648 | tf_op jit(solution)/shard_map/convert_element_type | solution.py:289
